TPU v7x, 32 devices: a whole 2x2x4 slice. The times are simulated.
32 devices in a mesh: paths: 4 (over y, core), contract: 8 (over z, x).
Axes of the slice: x: 2, y: 2, z: 4, core: 2. Of those that a mesh axis runs over, the one named last changes fastest.
Arguments:
- prices: float32 [1, 512], P(None, 'paths'), may hold values from -6 to 6
- terminal: bfloat16 [128, 512, 128], P('contract', 'paths'), may hold values from -6 to 6
- band: int32 [128], replicated, may hold values from 32 to 128
- position: int32 [128], replicated, may hold values from 0 to 127, as said below
- actions: int32 [128, 3], replicated, may hold values from -3 to 3
- degree: int32 [128], replicated, may hold values from 2 to 7
- volume: float32 [128], replicated, may hold values from 0.05 to 0.5
Outputs:
- valued: bfloat16 [128, 512, 128], P('contract', 'paths')
Inputs may be any that keep to these rules, and one draw needn't show every extreme that they name: A permutation of the contracts; contract c goes to new block position[c] // 16. Each old block of 16 contracts sends exactly 2 contracts to each of the 8 new blocks.
All inputs are finite; a program needn't handle non-finite values.
Results may differ from a plain program's by a relative error of at most 0.0038.
Values may be sent and summed in bfloat16 or wider, within the bound.
No kernel may reach another device: no remote copies, remote signals or barrier semaphores. Data moves between devices by JAX's collectives and lax.ppermute only.
A program may use at most 64 MiB of HBM per device.

v0:
```python
import jax
import jax.numpy as jnp
from jax import lax
from jax.sharding import PartitionSpec as P

LEVELS = 128
BASIS = 8
MOVE = 3
RIDGE = 0.05
DISCOUNT = 0.98
SPOT_SCALE = 0.25


def chebyshev(prices_row):
    scaled = jnp.tanh(prices_row)
    series = [jnp.ones_like(scaled), scaled]
    for order in range(2, BASIS):
        series.append(2.0 * scaled * series[-1] - series[-2])
    return jnp.stack(series[:BASIS])


def regress(gram, moments, path_count, degree_block):
    orders = jnp.arange(BASIS, dtype=jnp.int32)
    keep_basis = (orders[None, :] <= degree_block[:, None]).astype(jnp.float32)
    identity = jnp.eye(BASIS, dtype=jnp.float32)
    system = keep_basis[:, :, None] * keep_basis[:, None, :] * (gram / path_count)[None]
    system = system + (1.0 - keep_basis)[:, :, None] * identity[None] + RIDGE * identity[None]
    scaled_moments = keep_basis[:, :, None] * (moments / path_count)
    factor = jnp.linalg.cholesky(system)
    halfway = lax.linalg.triangular_solve(factor, scaled_moments, left_side=True, lower=True)
    return lax.linalg.triangular_solve(
        factor, halfway, left_side=True, lower=True, transpose_a=True
    )


def decide(values_now, estimate, spot_price, band_block, action_block, volume_block):
    levels = jnp.arange(LEVELS, dtype=jnp.int32)
    living = levels[None, :] < band_block[:, None]
    padded = jnp.pad(estimate, ((0, 0), (0, 0), (MOVE, MOVE)))
    optimum = DISCOUNT * estimate
    for offset in range(-MOVE, MOVE + 1):
        if offset == 0:
            continue
        allowed = jnp.any(action_block == offset, axis=1)
        target_level = levels + offset
        inside = (target_level[None, :] >= 0) & (target_level[None, :] < band_block[:, None])
        moved = padded[:, :, MOVE + offset : MOVE + offset + LEVELS]
        candidate = (
            -offset * volume_block[:, None, None] * spot_price[None, :, None] + DISCOUNT * moved
        )
        usable = allowed[:, None, None] & inside[:, None, :]
        optimum = jnp.where(usable, jnp.maximum(optimum, candidate), optimum)
    return jnp.where(living[:, None, :], optimum + DISCOUNT * (values_now - estimate), 0.0)


def lookup_flat(contract_ids, table):
    matches = contract_ids[:, None] == jnp.arange(table.shape[0], dtype=jnp.int32)[None, :]
    return jnp.sum(jnp.where(matches, table[None, :], jnp.zeros((), table.dtype)), axis=1)


def lookup_rows(contract_ids, table):
    matches = contract_ids[:, None] == jnp.arange(table.shape[0], dtype=jnp.int32)[None, :]
    return jnp.sum(
        jnp.where(matches[:, :, None], table[None, :, :], jnp.zeros((), table.dtype)), axis=1
    )


def redistribute(grids, position, block_count, myself, capacity):
    con_count = grids.shape[0]
    slot_ids = jnp.arange(con_count, dtype=jnp.int32)
    target = position // con_count
    target_grid = target.reshape(block_count, con_count)
    mine = lax.dynamic_slice_in_dim(target, myself * con_count, con_count)
    earlier = slot_ids[None, :] < slot_ids[:, None]
    rank_out = jnp.sum(earlier & (mine[None, :] == mine[:, None]), axis=1)
    flat_slot = mine * capacity + rank_out
    send_slots = jnp.arange(block_count * capacity, dtype=jnp.int32)
    matches = flat_slot[None, :] == send_slots[:, None]
    source_row = jnp.sum(jnp.where(matches, slot_ids[None, :], 0), axis=1)
    filled = jnp.any(matches, axis=1)
    outgoing = jnp.where(filled[:, None, None], grids[source_row], jnp.zeros((), grids.dtype))
    outgoing = outgoing.reshape((block_count, capacity) + grids.shape[1:])
    incoming = lax.all_to_all(outgoing, "contract", split_axis=0, concat_axis=0, tiled=True)
    wanted = myself * con_count + slot_ids
    owner_match = position[None, :] == wanted[:, None]
    owner_ids = jnp.sum(
        jnp.where(owner_match, jnp.arange(position.shape[0], dtype=jnp.int32)[None, :], 0), axis=1
    )
    source_block = owner_ids // con_count
    source_slot = owner_ids % con_count
    block_match = source_block[:, None] == jnp.arange(block_count, dtype=jnp.int32)[None, :]
    peer_targets = jnp.sum(jnp.where(block_match[:, :, None], target_grid[None, :, :], 0), axis=1)
    rank_in = jnp.sum((slot_ids[None, :] < source_slot[:, None]) & (peer_targets == myself), axis=1)
    chosen = source_block * capacity + rank_in
    arrived = incoming.reshape((block_count * capacity,) + grids.shape[1:])[chosen]
    return (arrived, owner_ids)


def window(prices, values_now, contract_ids, band, actions, degree, volume, path_count):
    highest = lax.Precision.HIGHEST
    band_block = lookup_flat(contract_ids, band)
    degree_block = lookup_flat(contract_ids, degree)
    volume_block = lookup_flat(contract_ids, volume)
    action_block = lookup_rows(contract_ids, actions)
    basis_rows = chebyshev(prices[0])
    spot_price = jnp.exp(SPOT_SCALE * prices[0])
    gram_part = jnp.dot(basis_rows, basis_rows.T, precision=highest)
    moments = jnp.einsum("kp,cpl->ckl", basis_rows, values_now, precision=highest)
    gram = lax.psum(gram_part.astype(jnp.bfloat16), "paths").astype(jnp.float32)
    moments_all = lax.psum(moments.astype(jnp.bfloat16), "paths").astype(jnp.float32)
    fitted = regress(gram, moments_all, path_count, degree_block)
    estimate = jnp.einsum("kp,ckl->cpl", basis_rows, fitted, precision=highest)
    values_now = decide(values_now, estimate, spot_price, band_block, action_block, volume_block)
    return values_now


def per_device(prices, terminal, band, position, actions, degree, volume):
    block_count = lax.axis_size("contract")
    myself = lax.axis_index("contract")
    con_count = terminal.shape[0]
    capacity = con_count // block_count
    path_count = prices.shape[1] * lax.axis_size("paths")
    grids, contract_ids = redistribute(terminal, position, block_count, myself, capacity)
    values_now = window(
        prices, grids.astype(jnp.float32), contract_ids, band, actions, degree, volume, path_count
    )
    result = values_now.astype(jnp.bfloat16)
    return result


def solution(mesh):
    in_specs = (P(None, "paths"), P("contract", "paths", None), P(), P(), P(), P(), P())
    out_specs = P("contract", "paths", None)
    return jax.shard_map(
        per_device, mesh=mesh, in_specs=in_specs, out_specs=out_specs, check_vma=False
    )
```

profile of v0, /device:TPU:0, one launch (start us, length us, event | category | flops | bytes accessed | tf_op | source)
XLA Modules:
  0.0 64.9 jit_solution(13784414937052553500)
XLA Ops:
  0.0 0.7 %and_select_fusion.3 = s32[128]{0:T(128)S(1)} fusion(s32[128]{0:T(128)} %param.10), kind=kLoop, calls=%fused_computation.97 | loop fusion | flops 1920 | bytes 1024 | tf_op jit(solution)/shard_map/jit(floor_divide)/jit(_where)/select_n | solution.py:71
  0.8 0.2 convert_reduce_fusion.1
  1.0 0.1 multiply_add_fusion
  1.1 0.1 select_reduce_fusion.4
  1.2 0.1 fusion.25
  1.3 0.1 broadcast_in_dim.162
  1.4 0.6 gather_fusion
  2.1 0.9 %broadcast_select_fusion = bf16[8,2,128,128]{3,2,1,0:T(8,128)(2,1)} fusion(bf16[8,2,128,128]{3,2,1,0:T(8,128)(2,1)S(1)} %bitcast.48, pred[8,2]{1,0:T(8,128)(4,1)S(1)} %broadcast_in_dim.162), kind=kLoop, calls=%fused_computation.27 | loop fusion | flops 262144 | bytes 1048592 | tf_op jit(solution)/shard_map/jit(_where)/select_n | solution.py:81
  3.0 7.3 %all-to-all-start = ((bf16[8,2,128,128]{3,2,1,0:T(8,128)(2,1)}), bf16[8,2,128,128]{3,2,1,0:T(8,128)(2,1)S(1)}, u32[]{:S(2)}, u32[]{:S(2)}) async-start(bf16[8,2,128,128]{3,2,1,0:T(8,128)(2,1)} %broadcast_select_fusion), calls=%async_computation | async-start | bytes 1048576 | tf_op jit(solution)/shard_map/all_to_all | solution.py:83
  10.4 0.2 select_reduce_fusion.7
  10.8 0.2 select_reduce_fusion.3
  11.1 0.1 select_reduce_fusion.2
  11.3 0.1 select_reduce_fusion
  11.4 0.2 convert_reduce_fusion
  11.6 0.2 select_reduce_fusion.6
  11.9 0.1 convolution_convert_fusion.1
  12.1 0.1 iota_compare_fusion.6
  12.2 0.1 broadcast_multiply_fusion.5
  12.3 12.5 %all-to-all-done = bf16[8,2,128,128]{3,2,1,0:T(8,128)(2,1)S(1)} async-done(((bf16[8,2,128,128]{3,2,1,0:T(8,128)(2,1)}), bf16[8,2,128,128]{3,2,1,0:T(8,128)(2,1)S(1)}, u32[]{:S(2)}, u32[]{:S(2)}) %all-to-all-start) | async-done | bytes 524320 | tf_op jit(solution)/shard_map/all_to_all | solution.py:83
  24.8 0.6 gather_fusion.1
  25.5 0.3 fusion
  25.8 0.3 copy.28
  26.1 10.5 %all-reduce.1 = (bf16[8,8]{1,0:T(8,128)(2,1)S(1)}, bf16[16,8,128]{2,1,0:T(8,128)(2,1)S(1)}) all-reduce(bf16[8,8]{1,0:T(8,128)(2,1)S(1)} %convolution_convert_fusion.1, bf16[16,8,128]{2,1,0:T(8,128)(2,1)S(1)} %fusion), channel_id=1, replica_groups=mesh['paths'=4,'contract'=8] {'paths'}, use_global_device_ids=true, to_apply=%region_10.11 | all-reduce | flops 16448 | bytes 65792 | tf_op jit(solution)/shard_map/psum | solution.py:109
  36.6 0.1 fusion.15
  36.8 11.7 %custom-call.9 = f32[16,8,8]{2,1,0:T(8,128)S(1)} custom-call(f32[16,8,8]{2,1,0:T(8,128)S(1)} %fusion.15), custom_call_target="Cholesky" | custom-call | tf_op jit(solution)/shard_map/jit(cholesky)/cholesky | solution.py:29
  48.6 0.1 select_bitcast_fusion
  48.7 10.0 %custom-call.10 = f32[16,1,8,8]{2,3,1,0:T(8,128)S(1)} custom-call(f32[16,1,8,8]{3,2,1,0:T(8,128)S(1)} %select_bitcast_fusion), custom_call_target="InvertDiagBlocksLowerTriangular" | custom-call | tf_op jit(solution)/shard_map/triangular_solve | solution.py:31
  58.8 0.4 fusion.20
  59.2 0.3 fusion.18
  59.4 1.8 %convolution_bitcast_fusion = f32[16,128,128]{1,2,0:T(8,128)S(1)} fusion(f32[16,8,128]{2,1,0:T(8,128)S(1)} %fusion.18, f32[8,128]{1,0:T(8,128)S(1)} %stack.2), kind=kOutput, calls=%fused_computation.8 | convolution fusion | flops 25165824 | bytes 1118208 | tf_op jit(solution)/shard_map/kp,ckl->cpl/dot_general | solution.py:112
  61.3 2.6 %fusion.11 = bf16[16,128,128]{1,2,0:T(8,128)(2,1)S(1)} fusion(f32[16,128,128]{1,2,0:T(8,128)S(1)} %convolution_bitcast_fusion, bf16[16,128,128]{1,2,0:T(8,128)(2,1)S(1)} %copy.28, f32[16,128]{1,0:T(8,128)S(1)} %get-tuple-element.34, f32[16,128]{1,0:T(8,128)S(1)} %get-tuple-element.33, f32[16,128]{1,0:T(8,128)S(1)} %get-tuple-element.32, ...), kind=kLoop, calls=%fused_computation.26 | loop fusion | flops 8126464 | bytes 2160640 | tf_op jit(solution)/shard_map/convert_element_type | solution.py:127
  63.9 1.0 %copy.29 = bf16[16,128,128]{2,1,0:T(8,128)(2,1)} copy(bf16[16,128,128]{1,2,0:T(8,128)(2,1)S(1)} %fusion.11) | data formatting | bytes 1048576 | tf_op jit(solution)/shard_map/convert_element_type | solution.py:127
  (47 shorter events, 0.9 us)
Async XLA Ops:
  0.0 1.4 %copy-start = (bf16[16,128,128]{2,1,0:T(8,128)(2,1)S(1)}, bf16[16,128,128]{2,1,0:T(8,128)(2,1)}, u32[]{:S(2)}) copy-start(bf16[16,128,128]{2,1,0:T(8,128)(2,1)} %param.8) | copy-start | bytes 1572868
  2.1 8.3 %copy-start.5 = (s32[128]{0:T(128)S(1)}, s32[128]{0:T(128)}, u32[]{:S(2)}) copy-start(s32[128]{0:T(128)} %param.10) | copy-start | bytes 1540
  2.1 8.7 %copy-start.6 = (f32[128]{0:T(128)S(1)}, f32[128]{0:T(128)}, u32[]{:S(2)}) copy-start(f32[128]{0:T(128)} %param.13) | copy-start | bytes 1540
  2.1 9.0 %copy-start.1 = (s32[128,3]{0,1:T(4,128)S(1)}, s32[128,3]{0,1:T(4,128)}, u32[]{:S(2)}) copy-start(s32[128,3]{0,1:T(4,128)} %param.11) | copy-start | bytes 4612
  2.1 9.1 %copy-start.2 = (f32[1,128]{1,0:T(1,128)S(1)}, f32[1,128]{1,0:T(1,128)}, u32[]{:S(2)}) copy-start(f32[1,128]{1,0:T(1,128)} %param.7) | copy-start | bytes 1540
  2.1 9.5 %copy-start.3 = (s32[128]{0:T(128)S(1)}, s32[128]{0:T(128)}, u32[]{:S(2)}) copy-start(s32[128]{0:T(128)} %param.9) | copy-start | bytes 1540
  2.1 9.5 %copy-start.4 = (s32[128]{0:T(128)S(1)}, s32[128]{0:T(128)}, u32[]{:S(2)}) copy-start(s32[128]{0:T(128)} %param.12) | copy-start | bytes 1540
  3.0 21.8 %all-to-all-start = ((bf16[8,2,128,128]{3,2,1,0:T(8,128)(2,1)}), bf16[8,2,128,128]{3,2,1,0:T(8,128)(2,1)S(1)}, u32[]{:S(2)}, u32[]{:S(2)}) async-start(bf16[8,2,128,128]{3,2,1,0:T(8,128)(2,1)} %broadcast_select_fusion), calls=%async_computation | async-start | bytes 1048576 | tf_op jit(solution)/shard_map/all_to_all | solution.py:83
where the time goes:
time: 65.1 us; the launch traced here: 64.9 us
  other arithmetic  28.4 us (44%)
  waiting for transfers between devices  12.5 us (19%)
  blocking collectives  10.5 us (16%)
  starting transfers between devices  7.28 us (11%)
  local copies, waits for them, and re-layouts  3.04 us (5%)
  matrix products  2.92 us (4%)
    all_to_all x1, waiting for transfers between devices, redistribute(): lax.all_to_all(outgoing, 'contract', split_axis=0, concat_axis=0, tiled=T...  12.5 us
    another operation x4, other arithmetic, regress(): factor = jnp.linalg.cholesky(system)  11.8 us
    psum x1, blocking collectives, window(): gram = lax.psum(gram_part.astype(jnp.bfloat16), 'paths').astype(jnp.float32)  10.5 us
    another operation x3, other arithmetic, regress(): lax.linalg.triangular_solve(factor, halfway, left_side=True, lower=True,...  10.1 us
    all_to_all x1, starting transfers between devices, redistribute(): lax.all_to_all(outgoing, 'contract', split_axis=0, concat_axis=0, tiled=T...  7.28 us
    convert_element_type x1, other arithmetic, per_device(): result = values_now.astype(jnp.bfloat16)  2.63 us
    dot_general x1, matrix products, window(): estimate = jnp.einsum('kp,ckl->cpl', basis_rows, fitted, precision=highest)  1.81 us
  transfers between devices with their start and end apart: 1, of which 1 were waited for; matrix products, arithmetic and copies ran while one was open for 3% of the time, Pallas kernels for 0%

commit v1 on v0

--- a/solution.py
+++ b/solution.py
@@ -9,6 +9,12 @@
 RIDGE = 0.05
 DISCOUNT = 0.98
 SPOT_SCALE = 0.25
+
+
+def add_all(x, name):
+    parts = lax.all_gather(x, name, axis=0, tiled=False)
+    summed = parts.sum(axis=0)
+    return summed
 
 
 def chebyshev(prices_row):
@@ -106,7 +112,7 @@
     spot_price = jnp.exp(SPOT_SCALE * prices[0])
     gram_part = jnp.dot(basis_rows, basis_rows.T, precision=highest)
     moments = jnp.einsum("kp,cpl->ckl", basis_rows, values_now, precision=highest)
-    gram = lax.psum(gram_part.astype(jnp.bfloat16), "paths").astype(jnp.float32)
+    gram = add_all(gram_part.astype(jnp.bfloat16), "paths").astype(jnp.float32)
     moments_all = lax.psum(moments.astype(jnp.bfloat16), "paths").astype(jnp.float32)
     fitted = regress(gram, moments_all, path_count, degree_block)
     estimate = jnp.einsum("kp,ckl->cpl", basis_rows, fitted, precision=highest)

time: 65.1 us -> 59.1 us (0.908)
  waiting for transfers between devices: 12.5 us -> 0.01 us
  blocking collectives: 10.5 us -> 16.8 us
    all_to_all x1, waiting for transfers between devices: 12.5 us -> 0.01 us  [redistribute(): lax.all_to_all(outgoing, 'contract', split_axis=0, concat_axis=0, tiled=T...]
    all_gather x0 -> x1, blocking collectives: none -> 5.19 us  [add_all(): parts = lax.all_gather(x, name, axis=0, tiled=False)]
    psum x1, blocking collectives: 10.5 us -> 11.6 us  [window(): lax.psum(moments.astype(jnp.bfloat16), 'paths').astype(jnp.float32)]
  transfers between devices with their start and end apart: 1 -> 1, of which waited for: 1 -> 0; matrix products, arithmetic and copies ran while one was open for 3% -> 41% of each run, Pallas kernels for 0% -> 0%
where the time goes in v1:
time: 59.1 us; the launch traced here: 58.9 us
  other arithmetic  28.4 us (48%)
  blocking collectives  16.8 us (28%)
  starting transfers between devices  7.41 us (13%)
  local copies, waits for them, and re-layouts  3.04 us (5%)
  matrix products  2.84 us (5%)
    another operation x4, other arithmetic, regress(): factor = jnp.linalg.cholesky(system)  11.8 us
    psum x1, blocking collectives, window(): lax.psum(moments.astype(jnp.bfloat16), 'paths').astype(jnp.float32)  11.6 us
    another operation x3, other arithmetic, regress(): lax.linalg.triangular_solve(factor, halfway, left_side=True, lower=True,...  10.1 us
    all_to_all x1, starting transfers between devices, redistribute(): lax.all_to_all(outgoing, 'contract', split_axis=0, concat_axis=0, tiled=T...  7.41 us
    all_gather x1, blocking collectives, add_all(): parts = lax.all_gather(x, name, axis=0, tiled=False)  5.19 us
    convert_element_type x1, other arithmetic, per_device(): result = values_now.astype(jnp.bfloat16)  2.62 us
    dot_general x1, matrix products, window(): estimate = jnp.einsum('kp,ckl->cpl', basis_rows, fitted, precision=highest)  1.81 us
  transfers between devices with their start and end apart: 1, of which 0 were waited for; matrix products, arithmetic and copies ran while one was open for 41% of the time, Pallas kernels for 0%

profile of v1, /device:TPU:0, one launch (start us, length us, event | category | flops | bytes accessed | tf_op | source)
XLA Modules:
  0.0 58.9 jit_solution(2211462672738641033)
XLA Ops:
  0.0 0.7 %and_select_fusion.3 = s32[128]{0:T(128)S(1)} fusion(s32[128]{0:T(128)} %param.10), kind=kLoop, calls=%fused_computation.98 | loop fusion | flops 1920 | bytes 1024 | tf_op jit(solution)/shard_map/jit(floor_divide)/jit(_where)/select_n | solution.py:77
  0.8 0.2 convert_reduce_fusion.1
  1.1 0.1 select_reduce_fusion.4
  1.2 0.1 fusion.25
  1.3 0.1 broadcast_in_dim.162
  1.4 0.6 %gather_fusion = bf16[16,128,128]{2,1,0:T(8,128)(2,1)S(1)} fusion(bf16[16,128,128]{2,1,0:T(8,128)(2,1)S(1)} %copy-done, s32[1024]{0:T(1024)S(1)} %pad_clamp_fusion.1), kind=kCustom, calls=%fused_computation | custom fusion | bytes 1048640 | tf_op jit(solution)/shard_map/gather | solution.py:87
  2.1 0.9 %broadcast_select_fusion = bf16[8,2,128,128]{3,2,1,0:T(8,128)(2,1)} fusion(bf16[8,2,128,128]{3,2,1,0:T(8,128)(2,1)S(1)} %bitcast.50, pred[8,2]{1,0:T(8,128)(4,1)S(1)} %broadcast_in_dim.162), kind=kLoop, calls=%fused_computation.27 | loop fusion | flops 262144 | bytes 1048592 | tf_op jit(solution)/shard_map/jit(_where)/select_n | solution.py:87
  3.0 7.4 %all-to-all-start = ((bf16[8,2,128,128]{3,2,1,0:T(8,128)(2,1)}), bf16[8,2,128,128]{3,2,1,0:T(8,128)(2,1)S(1)}, u32[]{:S(2)}, u32[]{:S(2)}) async-start(bf16[8,2,128,128]{3,2,1,0:T(8,128)(2,1)} %broadcast_select_fusion), calls=%async_computation | async-start | bytes 1048576 | tf_op jit(solution)/shard_map/all_to_all | solution.py:89
  10.5 0.2 select_reduce_fusion.7
  10.9 0.2 select_reduce_fusion.6
  11.4 0.1 convolution_convert_fusion.1
  11.5 0.1 select_reduce_fusion
  11.7 0.2 convert_reduce_fusion
  11.9 5.2 %all-gather = bf16[32,8]{1,0:T(8,128)(2,1)S(1)} all-gather(bf16[8,8]{1,0:T(8,128)(2,1)S(1)} %convolution_convert_fusion.1), channel_id=2, replica_groups=mesh['paths'=4,'contract'=8] {'paths'}, dimensions={0}, use_global_device_ids=true | all-gather | bytes 640 | tf_op jit(solution)/shard_map/all_gather | solution.py:15
  17.2 0.1 fusion.15
  17.3 11.7 %custom-call.9 = f32[16,8,8]{2,1,0:T(8,128)S(1)} custom-call(f32[16,8,8]{2,1,0:T(8,128)S(1)} %fusion.15), custom_call_target="Cholesky" | custom-call | tf_op jit(solution)/shard_map/jit(cholesky)/cholesky | solution.py:35
  29.2 0.1 select_reduce_fusion.2
  29.3 0.1 select_bitcast_fusion
  29.4 10.0 %custom-call.10 = f32[16,1,8,8]{2,3,1,0:T(8,128)S(1)} custom-call(f32[16,1,8,8]{3,2,1,0:T(8,128)S(1)} %select_bitcast_fusion), custom_call_target="InvertDiagBlocksLowerTriangular" | custom-call | tf_op jit(solution)/shard_map/triangular_solve | solution.py:37
  39.4 0.1 compare_reduce_fusion.6
  39.5 0.2 select_reduce_fusion.3
  39.7 0.1 iota_compare_fusion.6
  39.8 0.1 broadcast_multiply_fusion.5
  39.9 0.6 %gather_fusion.1 = bf16[16,128,128]{2,1,0:T(8,128)(2,1)S(1)} fusion(bf16[16,128,128]{2,1,0:T(8,128)(2,1)S(1)} %bitcast.49, s32[1024]{0:T(1024)S(1)} %pad_clamp_fusion), kind=kCustom, calls=%fused_computation.1 | custom fusion | bytes 1048640 | tf_op jit(solution)/shard_map/gather | solution.py:101
  40.6 0.3 fusion
  40.9 0.3 copy.33
  41.2 11.6 %psum.7 = bf16[16,8,128]{2,1,0:T(8,128)(2,1)S(1)} all-reduce(bf16[16,8,128]{2,1,0:T(8,128)(2,1)S(1)} %fusion), channel_id=1, replica_groups=mesh['paths'=4,'contract'=8] {'paths'}, use_global_device_ids=true, to_apply=%region_18.19 | all-reduce | flops 16384 | bytes 65536 | tf_op jit(solution)/shard_map/psum | solution.py:116
  52.8 0.3 fusion.20
  53.2 0.3 fusion.18
  53.4 1.8 %convolution_bitcast_fusion = f32[16,128,128]{1,2,0:T(8,128)S(1)} fusion(f32[16,8,128]{2,1,0:T(8,128)S(1)} %fusion.18, f32[8,128]{1,0:T(8,128)S(1)} %stack.2), kind=kOutput, calls=%fused_computation.8 | convolution fusion | flops 25165824 | bytes 1118208 | tf_op jit(solution)/shard_map/kp,ckl->cpl/dot_general | solution.py:118
  55.2 2.6 %fusion.11 = bf16[16,128,128]{1,2,0:T(8,128)(2,1)S(1)} fusion(f32[16,128,128]{1,2,0:T(8,128)S(1)} %convolution_bitcast_fusion, bf16[16,128,128]{1,2,0:T(8,128)(2,1)S(1)} %copy.33, f32[16,128]{1,0:T(8,128)S(1)} %get-tuple-element.32, f32[16,128]{1,0:T(8,128)S(1)} %get-tuple-element.31, f32[16,128]{1,0:T(8,128)S(1)} %get-tuple-element.30, ...), kind=kLoop, calls=%fused_computation.26 | loop fusion | flops 8126464 | bytes 2160640 | tf_op jit(solution)/shard_map/convert_element_type | solution.py:133
  57.9 1.0 %copy.34 = bf16[16,128,128]{2,1,0:T(8,128)(2,1)} copy(bf16[16,128,128]{1,2,0:T(8,128)(2,1)S(1)} %fusion.11) | data formatting | bytes 1048576 | tf_op jit(solution)/shard_map/convert_element_type | solution.py:133
  (49 shorter events, 1.0 us)
Async XLA Ops:
  0.0 1.4 %copy-start = (bf16[16,128,128]{2,1,0:T(8,128)(2,1)S(1)}, bf16[16,128,128]{2,1,0:T(8,128)(2,1)}, u32[]{:S(2)}) copy-start(bf16[16,128,128]{2,1,0:T(8,128)(2,1)} %param.8) | copy-start | bytes 1572868
  2.1 8.5 %copy-start.5 = (s32[128]{0:T(128)S(1)}, s32[128]{0:T(128)}, u32[]{:S(2)}) copy-start(s32[128]{0:T(128)} %param.10) | copy-start | bytes 1540
  2.1 8.8 %copy-start.3 = (s32[128]{0:T(128)S(1)}, s32[128]{0:T(128)}, u32[]{:S(2)}) copy-start(s32[128]{0:T(128)} %param.9) | copy-start | bytes 1540
  2.1 8.8 %copy-start.4 = (s32[128]{0:T(128)S(1)}, s32[128]{0:T(128)}, u32[]{:S(2)}) copy-start(s32[128]{0:T(128)} %param.12) | copy-start | bytes 1540
  2.1 9.2 %copy-start.2 = (f32[1,128]{1,0:T(1,128)S(1)}, f32[1,128]{1,0:T(1,128)}, u32[]{:S(2)}) copy-start(f32[1,128]{1,0:T(1,128)} %param.7) | copy-start | bytes 1540
  2.1 27.0 %copy-start.1 = (s32[128,3]{0,1:T(4,128)S(1)}, s32[128,3]{0,1:T(4,128)}, u32[]{:S(2)}) copy-start(s32[128,3]{0,1:T(4,128)} %param.11) | copy-start | bytes 4612
  3.0 36.5 %copy-start.6 = (f32[128]{0:T(128)S(1)}, f32[128]{0:T(128)}, u32[]{:S(2)}) copy-start(f32[128]{0:T(128)} %param.13) | copy-start | bytes 1540
  3.0 36.9 %all-to-all-start = ((bf16[8,2,128,128]{3,2,1,0:T(8,128)(2,1)}), bf16[8,2,128,128]{3,2,1,0:T(8,128)(2,1)S(1)}, u32[]{:S(2)}, u32[]{:S(2)}) async-start(bf16[8,2,128,128]{3,2,1,0:T(8,128)(2,1)} %broadcast_select_fusion), calls=%async_computation | async-start | bytes 1048576 | tf_op jit(solution)/shard_map/all_to_all | solution.py:89
